TPU v7x, 8 devices: a whole 2x2x1 slice. The times are simulated.
8 devices in a mesh: dp: 1 (over z), fsdp: 8 (over y, x, core).
Axes of the slice: x: 2, y: 2, z: 1, core: 2. Of those that a mesh axis runs over, the one named last changes fastest.
Arguments:
- dec_in: bfloat16 [64, 192, 4096], P(('dp', 'fsdp'))
- enc_out: bfloat16 [64, 384, 4096], P(('dp', 'fsdp'))
- dec_mask: int32 [64, 192], P(('dp', 'fsdp'))
- enc_mask: int32 [64, 384], P(('dp', 'fsdp'))
- rel_bias: float32 [32, 64], replicated
- norm_self: bfloat16 [4096], P('fsdp')
- self_q: bfloat16 [4096, 4096], P('fsdp')
- self_k: bfloat16 [4096, 4096], P('fsdp')
- self_v: bfloat16 [4096, 4096], P('fsdp')
- self_o: bfloat16 [4096, 4096], P('fsdp')
- norm_cross: bfloat16 [4096], P('fsdp')
- cross_q: bfloat16 [4096, 4096], P('fsdp')
- cross_k: bfloat16 [4096, 4096], P('fsdp')
- cross_v: bfloat16 [4096, 4096], P('fsdp')
- cross_o: bfloat16 [4096, 4096], P('fsdp')
- norm_ff: bfloat16 [4096], P('fsdp')
- ff_gate: bfloat16 [4096, 10240], P('fsdp')
- ff_lin: bfloat16 [4096, 10240], P('fsdp')
- ff_out: bfloat16 [10240, 4096], P('fsdp')
Outputs:
- output: bfloat16 [64, 192, 4096], P(('dp', 'fsdp'))
All inputs are finite; a program needn't handle non-finite values.
Results may differ from a plain program's by a relative error of at most 0.0177488.
Values are sent between devices in bfloat16 or wider.
A program may use at most 1 GiB of HBM per device.

v0:
```python
import math
import jax
import jax.numpy as jnp
from jax import lax
from jax.sharding import PartitionSpec as P, NamedSharding

HEAD_DIM = 64
NUM_BUCKETS = 32
EXACT_BUCKETS = 16
MAX_DISTANCE = 128
NORM_EPS = 1e-6
MASK_FILL = -1e9


def bucket_ids(length):
    return [offset if offset < EXACT_BUCKETS else min(NUM_BUCKETS - 1, EXACT_BUCKETS + int(math.log(offset / EXACT_BUCKETS) / math.log(MAX_DISTANCE / EXACT_BUCKETS) * (NUM_BUCKETS - EXACT_BUCKETS))) for offset in range(length)]


def rms_norm(values, scale_vec):
    val_f = values.astype(jnp.float32)
    mean_sq = jnp.mean(val_f * val_f, axis=-1, keepdims=True)
    return (val_f * lax.rsqrt(mean_sq + NORM_EPS) * scale_vec.astype(jnp.float32)).astype(jnp.bfloat16)


def project(hidden_in, weight):
    return jnp.einsum('btd,de->bte', hidden_in, weight, preferred_element_type=jnp.float32).astype(jnp.bfloat16)


def split_heads(hidden_in):
    return hidden_in.reshape(hidden_in.shape[0], hidden_in.shape[1], hidden_in.shape[2] // HEAD_DIM, HEAD_DIM)


def add_residual(residual, update):
    return (residual.astype(jnp.float32) + update.astype(jnp.float32)).astype(jnp.bfloat16)


def self_bias(rel_bias, tgt_len):
    positions = jnp.arange(tgt_len)
    rel_dist = jnp.maximum(positions[:, None] - positions[None, :], 0)
    bucket_table = jnp.array(bucket_ids(tgt_len), dtype=jnp.int32)
    per_offset = jnp.take(rel_bias, bucket_table, axis=0).T
    bias_heads = jnp.take(per_offset, rel_dist, axis=1)
    return jnp.where(positions[None, :] <= positions[:, None], bias_heads, MASK_FILL)


def attend(q_heads, k_heads, v_heads, add_bias, key_mask):
    scores = jnp.einsum('bqhd,bkhd->bhqk', q_heads, k_heads, preferred_element_type=jnp.float32) + add_bias
    scores = jnp.where(key_mask[:, None, None, :] > 0, scores, MASK_FILL)
    attn_prob = jax.nn.softmax(scores, axis=-1).astype(jnp.bfloat16)
    attn_ctx = jnp.einsum('bhqk,bkhd->bqhd', attn_prob, v_heads, preferred_element_type=jnp.float32).astype(jnp.bfloat16)
    return attn_ctx.reshape(attn_ctx.shape[0], attn_ctx.shape[1], -1)


def gather_full(w_shard):
    return lax.all_gather(w_shard, 'fsdp', axis=0, tiled=True)


def local_layer(dec_in, enc_out, dec_mask, enc_mask, rel_bias, norm_self, self_q, self_k, self_v, self_o, norm_cross, cross_q, cross_k, cross_v, cross_o, norm_ff, ff_gate, ff_lin, ff_out):
    bias_heads = self_bias(rel_bias, dec_in.shape[1])
    h_self = rms_norm(dec_in, gather_full(norm_self))
    q_self = split_heads(project(h_self, gather_full(self_q)))
    k_self = split_heads(project(h_self, gather_full(self_k)))
    v_self = split_heads(project(h_self, gather_full(self_v)))
    ctx_self = attend(q_self, k_self, v_self, bias_heads, dec_mask)
    x_one = add_residual(dec_in, project(ctx_self, gather_full(self_o)))
    h_cross = rms_norm(x_one, gather_full(norm_cross))
    q_cross = split_heads(project(h_cross, gather_full(cross_q)))
    k_cross = split_heads(project(enc_out, gather_full(cross_k)))
    v_cross = split_heads(project(enc_out, gather_full(cross_v)))
    ctx_cross = attend(q_cross, k_cross, v_cross, 0.0, enc_mask)
    x_two = add_residual(x_one, project(ctx_cross, gather_full(cross_o)))
    h_ff = rms_norm(x_two, gather_full(norm_ff))
    gate_act = project(h_ff, gather_full(ff_gate)).astype(jnp.float32)
    lin_act = project(h_ff, gather_full(ff_lin)).astype(jnp.float32)
    hidden = (jax.nn.gelu(gate_act, approximate=True) * lin_act).astype(jnp.bfloat16)
    return add_residual(x_two, project(hidden, gather_full(ff_out)))


def solution(mesh):
    row_spec = P(('dp', 'fsdp'), None, None)
    mask_spec = P(('dp', 'fsdp'), None)
    weight_spec = P('fsdp', None)
    scale_spec = P('fsdp')
    in_specs = (row_spec, row_spec, mask_spec, mask_spec, P(None, None), scale_spec, weight_spec, weight_spec, weight_spec, weight_spec, scale_spec, weight_spec, weight_spec, weight_spec, weight_spec, scale_spec, weight_spec, weight_spec, weight_spec)
    return jax.shard_map(local_layer, mesh=mesh, in_specs=in_specs, out_specs=row_spec, check_vma=False)
```

profile of v0, /device:TPU:0, one launch (start us, length us, event | category | flops | bytes accessed | tf_op | source)
XLA Modules:
  0.0 2539.7 jit_solution(11669983636774482152)
XLA Ops:
  6.5 0.7 all-gather.17.cloned.1.call-update
  7.3 0.7 all-gather.19.cloned.1.call-update
  8.1 0.7 all-gather.15.cloned.1.call-update
  10.5 0.7 all-gather.23.cloned.1.call-update
  11.3 0.7 all-gather.29.cloned.1.call-update
  12.1 0.7 all-gather.33.cloned.1.call-update
  13.4 0.7 all-gather.35.cloned.1.call-update
  14.2 13.7 all-gather
  27.9 7.1 fusion.53
  35.2 0.7 gather_fusion
  35.9 121.8 %gather_fusion.1 = f32[36864,64]{1,0:T(8,128)} fusion(f32[64,192]{0,1:T(8,128)S(1)} %bitcast.105, s32[36864]{0:T(1024)S(1)} %broadcast_clamp_fusion), kind=kCustom, calls=%fused_computation.1 | custom fusion | bytes 19021824 | tf_op jit(solution)/shard_map/jit(_take)/gather | solution.py:42
  157.8 19.6 copy.44
  177.4 0.6 broadcast_compare_fusion.1
  178.0 10.9 all-gather.1
  188.9 0.6 convert_element_type.144
  189.5 0.6 broadcast_compare_fusion
  190.1 11.2 all-gather.2
  201.3 0.6 convert_element_type.145
  202.0 11.7 select_bitcast_fusion
  213.7 62.5 %fusion.94 = bf16[8,192,4096]{2,1,0:T(8,128)(2,1)} fusion(bf16[4096,4096]{1,0:T(8,128)(2,1)} %all-gather.17.cloned.1.call-done, bf16[8,192,4096]{2,1,0:T(8,128)(2,1)} %param.20, f32[4096]{0:T(1024)S(1)} %bitcast.116, f32[8,192]{1,0:T(8,128)S(1)} %add_rsqrt_fusion.2), kind=kOutput, calls=%fused_computation.89 | convolution fusion | flops 51571064832 | bytes 58742784 | tf_op jit(solution)/shard_map/btd,de->bte/dot_general | solution.py:26
  276.2 19.6 copy.42
  295.8 29.0 %all-gather.19.cloned.1.call-done = bf16[4096,4096]{1,0:T(8,128)(2,1)} async-done(((bf16[512,4096]{1,0:T(8,128)(2,1)}), bf16[4096,4096]{1,0:T(8,128)(2,1)}) %all-gather.19.cloned.1.call-update) | async-done | bytes 33554448 | tf_op jit(solution)/shard_map/all_gather | solution.py:55
  324.8 63.1 %fusion.97 = bf16[8,192,4096]{2,1,0:T(8,128)(2,1)} fusion(bf16[4096,4096]{1,0:T(8,128)(2,1)} %all-gather.19.cloned.1.call-done, bf16[8,192,4096]{2,1,0:T(8,128)(2,1)} %param.20, f32[4096]{0:T(1024)S(1)} %bitcast.117, f32[8,192]{1,0:T(8,128)S(1)} %add_rsqrt_fusion.2), kind=kOutput, calls=%fused_computation.90 | convolution fusion | flops 51571064832 | bytes 58742784 | tf_op jit(solution)/shard_map/btd,de->bte/dot_general | solution.py:26
  387.9 19.6 copy.43
  407.5 74.4 %all-gather.15.cloned.1.call-done = bf16[4096,4096]{1,0:T(8,128)(2,1)} async-done(((bf16[512,4096]{1,0:T(8,128)(2,1)}), bf16[4096,4096]{1,0:T(8,128)(2,1)}) %all-gather.15.cloned.1.call-update) | async-done | bytes 33554448 | tf_op jit(solution)/shard_map/all_gather | solution.py:55
  481.9 62.7 %fusion.91 = bf16[8,192,4096]{2,1,0:T(8,128)(2,1)} fusion(bf16[4096,4096]{1,0:T(8,128)(2,1)} %all-gather.15.cloned.1.call-done, bf16[8,192,4096]{2,1,0:T(8,128)(2,1)} %param.20, f32[4096]{0:T(1024)S(1)} %bitcast.118, f32[8,192]{1,0:T(8,128)S(1)} %add_rsqrt_fusion.2), kind=kOutput, calls=%fused_computation.88 | convolution fusion | flops 51571064832 | bytes 58742784 | tf_op jit(solution)/shard_map/btd,de->bte/dot_general | solution.py:26
  544.6 19.6 copy.41
  564.2 55.3 %fusion.118 = (f32[8,64,192]{2,1,0:T(8,128)S(1)}, f32[8,64,192,192]{2,3,1,0:T(8,128)}) fusion(f32[64,192,192]{1,2,0:T(8,128)} %select_bitcast_fusion, pred[8,192]{1,0:T(8,128)(4,1)S(1)} %copy-done.2, bf16[8,192,64,64]{1,3,2,0:T(8,128)(2,1)} %bitcast.106, bf16[8,192,64,64]{1,3,2,0:T(8,128)(2,1)} %bitcast.107), kind=kOutput, calls=%fused_computation.108 | convolution fusion | flops 2491416832 | bytes 110495232 | tf_op jit(solution)/shard_map/sub | solution.py:49
  619.5 43.5 %fusion.79 = bf16[8,64,64,192]{3,2,1,0:T(8,128)(2,1)} fusion(bf16[8,192,64,64]{1,3,2,0:T(8,128)(2,1)} %bitcast.112, f32[8,64,192,192]{2,3,1,0:T(8,128)} %get-tuple-element.6, f32[8,64,192]{2,1,0:T(8,128)S(1)} %get-tuple-element.5), kind=kOutput, calls=%fused_computation.87 | convolution fusion | flops 2459959296 | bytes 101056512 | tf_op jit(solution)/shard_map/bhqk,bkhd->bqhd/dot_general | solution.py:50
  663.0 64.8 %fusion.57 = (f32[8,192]{1,0:T(8,128)S(1)}, bf16[8,192,4096]{2,1,0:T(8,128)(2,1)}) fusion(bf16[8,192,4096]{1,2,0:T(8,128)(2,1)} %bitcast.120, bf16[4096,4096]{1,0:T(8,128)(2,1)} %all-gather.21.cloned.1.call-done, bf16[8,192,4096]{2,1,0:T(8,128)(2,1)} %param.20), kind=kOutput, calls=%fused_computation.71 | convolution fusion | flops 51589939200 | bytes 71309312 | tf_op jit(solution)/shard_map/btd,de->bte/dot_general | solution.py:26
  727.9 67.8 %all-gather.25.cloned.1.call-done = bf16[4096,4096]{1,0:T(8,128)(2,1)} async-done(((bf16[512,4096]{1,0:T(8,128)(2,1)}), bf16[4096,4096]{1,0:T(8,128)(2,1)}) %all-gather.25.cloned.1.call-update) | async-done | bytes 33554448 | tf_op jit(solution)/shard_map/all_gather | solution.py:55
  795.7 62.6 %fusion.102 = bf16[8,192,4096]{2,1,0:T(8,128)(2,1)} fusion(bf16[4096,4096]{1,0:T(8,128)(2,1)} %all-gather.25.cloned.1.call-done, bf16[8,192,4096]{2,1,0:T(8,128)(2,1)} %get-tuple-element.8, f32[4096]{0:T(1024)S(1)} %bitcast.115, f32[8,192]{1,0:T(8,128)S(1)} %add_rsqrt_fusion.1), kind=kOutput, calls=%fused_computation.91 | convolution fusion | flops 51571064832 | bytes 58742784 | tf_op jit(solution)/shard_map/btd,de->bte/dot_general | solution.py:26
  858.3 19.6 copy.48
  877.9 74.7 %all-gather.27.cloned.1.call-done = bf16[4096,4096]{1,0:T(8,128)(2,1)} async-done(((bf16[512,4096]{1,0:T(8,128)(2,1)}), bf16[4096,4096]{1,0:T(8,128)(2,1)}) %all-gather.27.cloned.1.call-update) | async-done | bytes 33554448 | tf_op jit(solution)/shard_map/all_gather | solution.py:55
  952.6 114.9 %fusion.72 = bf16[8,384,4096]{2,1,0:T(8,128)(2,1)} fusion(bf16[8,384,4096]{2,1,0:T(8,128)(2,1)} %param.21, bf16[4096,4096]{1,0:T(8,128)(2,1)} %all-gather.27.cloned.1.call-done), kind=kOutput, calls=%fused_computation.82 | convolution fusion | flops 103091798016 | bytes 83886080 | tf_op jit(solution)/shard_map/btd,de->bte/dot_general | solution.py:26
  1067.5 32.7 %copy.49 = bf16[8,384,4096]{1,2,0:T(8,128)(2,1)} copy(bf16[8,384,4096]{2,1,0:T(8,128)(2,1)} %fusion.72) | data formatting | bytes 50331648 | tf_op jit(solution)/shard_map/convert_element_type | solution.py:26
  1100.2 9.5 all-gather.23.cloned.1.call-done
  1109.7 115.0 %fusion.69 = bf16[8,384,4096]{2,1,0:T(8,128)(2,1)} fusion(bf16[8,384,4096]{2,1,0:T(8,128)(2,1)} %param.21, bf16[4096,4096]{1,0:T(8,128)(2,1)} %all-gather.23.cloned.1.call-done), kind=kOutput, calls=%fused_computation.81 | convolution fusion | flops 103091798016 | bytes 83886080 | tf_op jit(solution)/shard_map/btd,de->bte/dot_general | solution.py:26
  1224.6 32.6 %copy.47 = bf16[8,384,4096]{1,2,0:T(8,128)(2,1)} copy(bf16[8,384,4096]{2,1,0:T(8,128)(2,1)} %fusion.69) | data formatting | bytes 50331648 | tf_op jit(solution)/shard_map/convert_element_type | solution.py:26
  1257.3 72.6 %fusion.119 = (f32[8,64,192]{2,1,0:T(8,128)S(1)}, f32[8,64,192,384]{3,2,1,0:T(8,128)}) fusion(pred[8,384]{1,0:T(8,128)(4,1)S(1)} %copy-done.7, bf16[8,192,64,64]{1,3,2,0:T(8,128)(2,1)} %bitcast.111, bf16[8,384,64,64]{1,3,2,0:T(8,128)(2,1)} %bitcast.109), kind=kOutput, calls=%fused_computation.109 | convolution fusion | flops 4945084928 | bytes 189139968 | tf_op jit(solution)/shard_map/sub | solution.py:49
  1329.9 61.0 %fusion.78 = bf16[8,64,64,192]{3,2,1,0:T(8,128)(2,1)} fusion(bf16[8,384,64,64]{1,3,2,0:T(8,128)(2,1)} %bitcast.110, f32[8,64,192,384]{3,2,1,0:T(8,128)} %get-tuple-element.10, f32[8,64,192]{2,1,0:T(8,128)S(1)} %get-tuple-element.9), kind=kOutput, calls=%fused_computation.86 | convolution fusion | flops 4913627136 | bytes 189136896 | tf_op jit(solution)/shard_map/bhqk,bkhd->bqhd/dot_general | solution.py:50
  1390.9 64.8 %fusion.61 = (f32[8,192]{1,0:T(8,128)S(1)}, bf16[8,192,4096]{2,1,0:T(8,128)(2,1)}) fusion(bf16[8,192,4096]{1,2,0:T(8,128)(2,1)} %bitcast.119, bf16[4096,4096]{1,0:T(8,128)(2,1)} %all-gather.29.cloned.1.call-done, bf16[8,192,4096]{2,1,0:T(8,128)(2,1)} %get-tuple-element.8), kind=kOutput, calls=%fused_computation.75 | convolution fusion | flops 51589939200 | bytes 71309312 | tf_op jit(solution)/shard_map/btd,de->bte/dot_general | solution.py:26
  1455.7 181.5 %all-gather.33.cloned.1.call-done = bf16[4096,10240]{1,0:T(8,128)(2,1)} async-done(((bf16[512,10240]{1,0:T(8,128)(2,1)}), bf16[4096,10240]{1,0:T(8,128)(2,1)}) %all-gather.33.cloned.1.call-update) | async-done | bytes 83886096 | tf_op jit(solution)/shard_map/all_gather | solution.py:55
  1637.2 145.1 %fusion.7 = bf16[8,192,10240]{2,1,0:T(8,128)(2,1)} fusion(bf16[4096,10240]{1,0:T(8,128)(2,1)} %all-gather.33.cloned.1.call-done, bf16[8,192,4096]{2,1,0:T(8,128)(2,1)} %get-tuple-element.12, f32[4096]{0:T(1024)S(1)} %bitcast.113, f32[8,192]{1,0:T(8,128)S(1)} %add_rsqrt_fusion), kind=kOutput, calls=%fused_computation.17 | convolution fusion | flops 128874184704 | bytes 127948800 | tf_op jit(solution)/shard_map/btd,de->bte/dot_general | solution.py:26
  1782.4 225.2 %all-gather.31.cloned.1.call-done = bf16[4096,10240]{1,0:T(8,128)(2,1)} async-done(((bf16[512,10240]{1,0:T(8,128)(2,1)}), bf16[4096,10240]{1,0:T(8,128)(2,1)}) %all-gather.31.cloned.1.call-update) | async-done | bytes 83886096 | tf_op jit(solution)/shard_map/all_gather | solution.py:55
  2007.6 165.4 %fusion.151 = bf16[8,192,10240]{2,1,0:T(8,128)(2,1)} fusion(bf16[8,192,10240]{2,1,0:T(8,128)(2,1)} %fusion.7, bf16[4096,10240]{1,0:T(8,128)(2,1)} %all-gather.31.cloned.1.call-done, bf16[8,192,4096]{2,1,0:T(8,128)(2,1)} %get-tuple-element.12, f32[4096]{0:T(1024)S(1)} %bitcast.114, f32[8,192]{1,0:T(8,128)S(1)} %add_rsqrt_fusion), kind=kOutput, calls=%fused_computation.31.clone.clone.clone.clone.1 | convolution fusion | flops 129078657024 | bytes 159406080 | tf_op jit(solution)/shard_map/btd,de->bte/dot_general | solution.py:26
  2172.9 205.1 %all-gather.35.cloned.1.call-done = bf16[10240,4096]{1,0:T(8,128)(2,1)} async-done(((bf16[1280,4096]{1,0:T(8,128)(2,1)}), bf16[10240,4096]{1,0:T(8,128)(2,1)}) %all-gather.35.cloned.1.call-update) | async-done | bytes 83886096 | tf_op jit(solution)/shard_map/all_gather | solution.py:55
  2378.1 154.8 %fusion.64 = bf16[8,192,4096]{2,1,0:T(8,128)(2,1)} fusion(bf16[8,192,4096]{2,1,0:T(8,128)(2,1)} %get-tuple-element.12, bf16[10240,4096]{1,0:T(8,128)(2,1)} %all-gather.35.cloned.1.call-done, bf16[8,192,10240]{2,1,0:T(8,128)(2,1)} %fusion.151), kind=kOutput, calls=%fused_computation.78 | convolution fusion | flops 128880476160 | bytes 140509184 | tf_op jit(solution)/shard_map/btd,de->bte/dot_general | solution.py:26
  (54 shorter events, 2.8 us)
Async XLA Ops:
  6.5 28.7 %copy-start = (f32[32,64]{1,0:T(8,128)S(1)}, f32[32,64]{1,0:T(8,128)}, u32[]{:S(2)}) copy-start(f32[32,64]{1,0:T(8,128)} %param.24) | copy-start | bytes 24580
  6.5 207.1 %all-gather.17.cloned.1.call-start = ((), (), s32[]{:S(2)}) async-start(), calls=%async_computation.1 | async-start | bytes 37748736 | tf_op jit(solution)/shard_map/all_gather | solution.py:55
  7.3 317.5 %all-gather.19.cloned.1.call-start = ((), (), s32[]{:S(2)}) async-start(), calls=%async_computation.2 | async-start | bytes 37748736 | tf_op jit(solution)/shard_map/all_gather | solution.py:55
  8.0 473.9 %all-gather.15.cloned.1.call-start = ((), (), s32[]{:S(2)}) async-start(), calls=%async_computation | async-start | bytes 37748736 | tf_op jit(solution)/shard_map/all_gather | solution.py:55
  8.7 654.3 %all-gather.21.cloned.1.call-start = ((), (), s32[]{:S(2)}) async-start(), calls=%async_computation.3 | async-start | bytes 37748736 | tf_op jit(solution)/shard_map/all_gather | solution.py:55
  9.3 4.8 copy-start.8
  9.3 786.4 %all-gather.25.cloned.1.call-start = ((), (), s32[]{:S(2)}) async-start(), calls=%async_computation.5 | async-start | bytes 37748736 | tf_op jit(solution)/shard_map/all_gather | solution.py:55
  9.9 942.7 %all-gather.27.cloned.1.call-start = ((), (), s32[]{:S(2)}) async-start(), calls=%async_computation.6 | async-start | bytes 37748736 | tf_op jit(solution)/shard_map/all_gather | solution.py:55
  10.5 1099.2 %all-gather.23.cloned.1.call-start = ((), (), s32[]{:S(2)}) async-start(), calls=%async_computation.4 | async-start | bytes 37748736 | tf_op jit(solution)/shard_map/all_gather | solution.py:55
  11.2 23.9 copy-start.11
  11.3 1379.6 %all-gather.29.cloned.1.call-start = ((), (), s32[]{:S(2)}) async-start(), calls=%async_computation.7 | async-start | bytes 37748736 | tf_op jit(solution)/shard_map/all_gather | solution.py:55
  12.0 1625.2 %all-gather.33.cloned.1.call-start = ((), (), s32[]{:S(2)}) async-start(), calls=%async_computation.9 | async-start | bytes 94371840 | tf_op jit(solution)/shard_map/all_gather | solution.py:55
  12.7 1994.8 %all-gather.31.cloned.1.call-start = ((), (), s32[]{:S(2)}) async-start(), calls=%async_computation.8 | async-start | bytes 94371840 | tf_op jit(solution)/shard_map/all_gather | solution.py:55
  13.3 2364.7 %all-gather.35.cloned.1.call-start = ((), (), s32[]{:S(2)}) async-start(), calls=%async_computation.10 | async-start | bytes 94371840 | tf_op jit(solution)/shard_map/all_gather | solution.py:55
  157.7 19.6 copy-start.6
  157.7 20.2 copy-start.9
  157.7 31.8 %copy-start.5 = (s32[8,384]{1,0:T(8,128)S(1)}, s32[8,384]{1,0:T(8,128)}, u32[]{:S(2)}) copy-start(s32[8,384]{1,0:T(8,128)} %param.23) | copy-start | bytes 36868
  157.7 32.4 %copy-start.10 = (bf16[512]{0:T(512)(128)(2,1)S(1)}, bf16[512]{0:T(512)(128)(2,1)}, u32[]{:S(2)}) copy-start(bf16[512]{0:T(512)(128)(2,1)} %param.35) | copy-start | bytes 3076
  544.6 19.6 copy-start.2
  663.0 132.7 %copy-start.4 = (f32[8,1,512]{2,1,0:T(1,128)S(1)}, f32[8,1,512]{2,1,0:T(1,128)}, u32[]{:S(2)}) copy-start(f32[8,1,512]{2,1,0:T(1,128)} %convert_element_type.144) | copy-start | bytes 49156
  1224.6 32.7 %copy-start.7 = (pred[8,384]{1,0:T(8,128)(4,1)S(1)}, pred[8,384]{1,0:T(8,128)(4,1)}, u32[]{:S(2)}) copy-start(pred[8,384]{1,0:T(8,128)(4,1)} %broadcast_compare_fusion) | copy-start | bytes 9220
  1390.9 246.3 %copy-start.3 = (f32[8,1,512]{2,1,0:T(1,128)S(1)}, f32[8,1,512]{2,1,0:T(1,128)}, u32[]{:S(2)}) copy-start(f32[8,1,512]{2,1,0:T(1,128)} %convert_element_type.145) | copy-start | bytes 49156
  2378.1 154.8 %copy-start.1 = (f32[32,64]{1,0:T(8,128)S(1)}, f32[32,64]{1,0:T(8,128)}, u32[]{:S(2)}) copy-start(f32[32,64]{1,0:T(8,128)} %param.24) | copy-start | bytes 24580
Sparse Core Ops, SparseCore 0:
  9.1 158.1 all-gather.16
  169.2 155.6 all-gather.18
  326.6 155.2 all-gather.14
  483.5 155.1 all-gather.20
  640.4 155.1 all-gather.24
  797.4 155.2 all-gather.26
  954.4 155.2 all-gather.22
  1111.5 155.2 all-gather.28
  1268.6 368.6 all-gather.32
  1638.9 368.5 all-gather.30
  2009.4 368.5 all-gather.34
where the time goes:
time: 2550 us; the launch traced here: 2540 us
  matrix products  1310 us (51%)
  waiting for transfers between devices  874 us (34%)
  local copies, waits for them, and re-layouts  286 us (11%)
  blocking collectives  35.8 us (1%)
    dot_general x11, matrix products, project(): jnp.einsum('btd,de->bte', hidden_in, weight, preferred_element_type=jnp.f...  1080 us
    all_gather x11, waiting for transfers between devices, gather_full(): return lax.all_gather(w_shard, 'fsdp', axis=0, tiled=True)  867 us
    convert_element_type x6, local copies, waits for them, and re-layouts, project(): jnp.einsum('btd,de->bte', hidden_in, weight, preferred_element_type=jnp.f...  144 us
    gather x2, local copies, waits for them, and re-layouts, self_bias(): bias_heads = jnp.take(per_offset, rel_dist, axis=1)  141 us
    sub x2, matrix products, attend(): attn_prob = jax.nn.softmax(scores, axis=-1).astype(jnp.bfloat16)  128 us
    dot_general x2, matrix products, attend(): jnp.einsum('bhqk,bkhd->bqhd', attn_prob, v_heads, preferred_element_type=...  104 us
  transfers between devices with their start and end apart: 11, of which 8 were waited for; matrix products, arithmetic and copies ran while one was open for 58% of the time, Pallas kernels for 0%

commit v1 on v0

v1 whole, which is shorter than its diff:
```python
import math
import jax
import jax.numpy as jnp
import numpy as np
from jax import lax
from jax.experimental import pallas as pl
from jax.experimental.pallas import tpu as pltpu
from jax.sharding import PartitionSpec as P

MESH = pl.DeviceIdType.MESH
F32, BF16 = jnp.float32, jnp.bfloat16
HEAD_DIM = 64
NUM_BUCKETS = 32
EXACT_BUCKETS = 16
MAX_DISTANCE = 128
NORM_EPS = 1e-6
MASK_FILL = -1e9
N_DEV = 8

AHEAD, PASS, DONE, RING = 4, 5, 6, 16
TASKS = {'self_q': 8, 'self_k': 8, 'self_v': 8, 'self_o': 8, 'cross_k': 8, 'cross_v': 8, 'cross_q': 8, 'cross_o': 8, 'ff_gate': 20, 'ff_lin': 20, 'ff_out': 16}
ALL_TASKS = sum(TASKS.values())
TICKS = {'head': 8, 'self_q': 8, 'self_k': 8, 'self_v': 8, 'self_attend': 6, 'self_o': 6, 'cross_k0': 6, 'cross_k1': 5, 'cross_v0': 6, 'cross_v1': 5,
         'cross_q': 6, 'cross_attend': 10, 'cross_o': 6, 'ff_gate': 13, 'ff_lin': 11, 'ff_out': 14}
assert sum(TICKS.values()) == ALL_TASKS + DONE
ROW_BLOCK = 512
GROUP = 512


def bucket_ids(length):
    return [offset if offset < EXACT_BUCKETS else min(NUM_BUCKETS - 1, EXACT_BUCKETS + int(math.log(offset / EXACT_BUCKETS) / math.log(MAX_DISTANCE / EXACT_BUCKETS) * (NUM_BUCKETS - EXACT_BUCKETS))) for offset in range(length)]


def bucket_row(length, lanes):
    ids = bucket_ids(length)
    return np.array([[ids[min((lanes - m) % lanes, length - 1)] for m in range(lanes)]], np.int32)


class Weight:
    def __init__(self, first, count, shard, got):
        self.first, self.count, self.shard, self.got = first, count, shard, got
        self.rows, self.width = shard.shape[0], shard.shape[1] // count


def layer_kernel(batch, names, buckets_ref, rel_ref, dec_mask_ref, enc_mask_ref, norm_ref, dec_ref, enc_ref, *refs):
    n_w = len(names)
    shards, refs = refs[:n_w], refs[n_w:]
    out_ref, q_ref, k_ref, v_ref, c_ref, ck_ref, cv_ref, g_ref, z_ref = refs[:9]
    gots, refs = refs[9:9 + n_w], refs[9 + n_w:]
    x_s, big, bias_s, dist_s, gain_in, gains, send_sem, recv_sem, norm_send, norm_recv, load_sem = refs

    me = lax.axis_index('fsdp')
    weights, first = {}, 0
    for name, shard, got in zip(names, shards, gots):
        weights[name] = Weight(first, TASKS[name], shard, got)
        first += TASKS[name]
    rows, width = dec_ref.shape
    tgt = rows // batch
    src = enc_ref.shape[0] // batch
    row_block = min(ROW_BLOCK, rows)

    def remote(src_ref, dst_ref, kind, ring, bit):
        return pltpu.make_async_remote_copy(src_ref=src_ref, dst_ref=dst_ref, send_sem=send_sem.at[kind, ring], recv_sem=recv_sem.at[kind, ring],
                                            device_id={'fsdp': me ^ bit}, device_id_type=MESH)

    class Task:
        def __init__(self, w, m, ring):
            cols = pl.ds(pl.multiple_of(m * w.width, w.width), w.width)
            own = w.shard.at[:, cols]
            slot = lambda j: w.got.at[j - 1, :, cols]
            low = lambda j: w.got.at[j - 1, pl.ds(0, w.rows // 2), cols]
            high = lambda j: w.got.at[j - 1, pl.ds(w.rows // 2, w.rows // 2), cols]
            self.to_partner = lambda: remote(own, slot(1), 0, ring, 1)
            self.to_x = lambda: remote(own, slot(2), 1, ring, 2)
            self.to_y = lambda: remote(own, slot(4), 2, ring, 4)
            self.relay_y = lambda: remote(low(2), low(6), 3, ring, 4)
            self.relay_x = lambda: remote(high(4), high(6), 4, ring, 2)
            self.swap_x = lambda: remote(slot(2), slot(3), 5, ring, 1)
            self.swap_y = lambda: remote(slot(4), slot(5), 6, ring, 1)
            self.swap_d = lambda: remote(slot(6), slot(7), 7, ring, 1)

    def send(t):
        for copy in (t.to_x, t.to_y, t.to_partner):
            copy().start()

    def arrive(t):
        t.to_partner().wait_recv()
        t.to_x().wait_recv()
        t.relay_y().start()
        t.swap_x().start()
        t.to_y().wait_recv()
        t.relay_x().start()
        t.swap_y().start()

    def pass_on(t):
        t.relay_y().wait_recv()
        t.relay_x().wait_recv()
        t.swap_d().start()

    def finish(t):
        for copy in (t.swap_x, t.swap_y, t.swap_d):
            copy().wait()
        for copy in (t.to_partner, t.to_x, t.to_y, t.relay_y, t.relay_x):
            copy().wait_send()

    def on_task(t, low, high, act):
        for w in weights.values():
            if low < w.first + w.count and w.first < high:
                def run(w=w):
                    act(Task(w, t - w.first, lax.rem(t, RING)))
                if w.first <= low and high <= w.first + w.count:
                    run()
                else:
                    pl.when((t >= w.first) & (t < w.first + w.count))(run)

    def tick(i, low, high):
        on_task(i, low, high, arrive)
        on_task(i + AHEAD, low + AHEAD, high + AHEAD, send)
        on_task(i - PASS, low - PASS, high - PASS, pass_on)
        on_task(i - DONE, low - DONE, high - DONE, finish)

    done = [0]

    def stage_ticks(name):
        low, count = done[0], TICKS[name]
        done[0] = low + count
        return low, count

    def run_ticks(plan, n, steps, one_each=False):
        low, count = plan
        if one_each:
            begin, end = jnp.minimum(low + n, low + count), jnp.minimum(low + n + 1, low + count)
        else:
            begin, end = low + (n * count) // steps, low + ((n + 1) * count) // steps

        @pl.loop(begin, end)
        def _(i):
            tick(i, low, low + count)

    def load(src_ref, dst_ref):
        copy = pltpu.make_async_copy(src_ref, dst_ref, load_sem)
        copy.start()
        copy.wait()

    def norm(which):
        @pl.loop(0, rows // 16)
        def _(r):
            span = pl.ds(pl.multiple_of(r * 16, 16), 16)
            v = x_s[span, :].astype(F32)
            scale = lax.rsqrt(jnp.mean(v * v, axis=-1, keepdims=True) + NORM_EPS)
            big[span, pl.ds(0, width)] = (v * scale * gains[pl.ds(which, 1), :]).astype(BF16)

    def matmul(name, stage, split, store, in_specs=(), ins=(), out_specs=(), outs=()):
        w = weights[name]
        steps, cols = w.count * split, w.width // split
        plan = stage_ticks(stage)

        def body(own, got, *rest):
            n = pl.program_id(0)

            @pl.loop(0, rows // row_block)
            def _(m):
                span = pl.ds(pl.multiple_of(m * row_block, row_block), row_block)
                total = None
                for j in range(N_DEV):
                    part = big[span, pl.ds(pl.multiple_of((me ^ j) * w.rows, 128), w.rows)]
                    term = jnp.dot(part, own[...] if j == 0 else got[j - 1], preferred_element_type=F32)
                    total = term if total is None else total + term
                store(total, span, n, *rest)

            run_ticks(plan, n, steps, stage == 'ff_out')

        pltpu.emit_pipeline(
            body, grid=(steps,),
            in_specs=[pl.BlockSpec((w.rows, cols), lambda n: (0, n)), pl.BlockSpec((N_DEV - 1, w.rows, cols), lambda n: (0, 0, n)), *in_specs],
            out_specs=list(out_specs))(w.shard, w.got, *ins, *outs)

    def project(name, stage, dst_ref, half=0):
        cols = weights[name].width

        def store(total, span, n, dst):
            dst[span, :] = total.astype(BF16)

        matmul(name, stage, 1, store, out_specs=[pl.BlockSpec((rows, cols), lambda n: (half, n))], outs=[dst_ref])

    def residual(name, stage):
        cols = weights[name].width

        def store(total, span, n):
            where = (span, pl.ds(pl.multiple_of(n * cols, cols), cols))
            x_s[where] = (x_s[where].astype(F32) + total.astype(BF16).astype(F32)).astype(BF16)

        matmul(name, stage, 1, store)

    left = lax.broadcasted_iota(jnp.int32, (tgt, 2 * HEAD_DIM), 1) < HEAD_DIM

    def softmax(scores):
        e = jnp.exp(scores - jnp.max(scores, axis=-1, keepdims=True))
        return (e * (1.0 / jnp.sum(e, axis=-1, keepdims=True))).astype(BF16)

    def attend(stage, keys, k_src, v_src, prepare, mask_scores):
        group = min(GROUP, width)
        plan = stage_ticks(stage)
        steps = (width // group) * batch

        def body(q, k, v, c):
            g, b = pl.program_id(0), pl.program_id(1)
            prepare(g, b)
            for pair in range(group // (2 * HEAD_DIM)):
                cols = pl.ds(pair * 2 * HEAD_DIM, 2 * HEAD_DIM)
                q_pair = q[:, cols].astype(F32)
                both = jnp.concatenate([jnp.where(left, q_pair, 0.0), jnp.where(left, 0.0, q_pair)], 0).astype(BF16)
                scores = lax.dot_general(both, k[:, cols], (((1,), (1,)), ((), ())), preferred_element_type=F32)
                prob = jnp.concatenate([softmax(mask_scores(scores[h * tgt:(h + 1) * tgt], 2 * pair + h, b)) for h in range(2)], 0)
                ctx = jnp.dot(prob, v[:, cols], preferred_element_type=F32)
                c[:, cols] = jnp.where(left, ctx[:tgt], ctx[tgt:]).astype(BF16)
            run_ticks(plan, g * batch + b, steps)

        spec = lambda length: pl.BlockSpec((length, group), lambda g, b: (b, g))
        pltpu.emit_pipeline(body, grid=(width // group, batch), in_specs=[spec(tgt), spec(keys), spec(keys)], out_specs=[spec(tgt)])(q_ref, k_src, v_src, c_ref)

    def self_attention():
        heads = min(GROUP, width) // HEAD_DIM
        causal = lax.broadcasted_iota(jnp.int32, (tgt, tgt), 1) <= lax.broadcasted_iota(jnp.int32, (tgt, tgt), 0)

        def prepare(g, b):
            @pl.when(b == 0)
            def _():
                @pl.loop(0, heads)
                def _(h):
                    row = jnp.broadcast_to(dist_s[pl.ds(g * heads + h, 1), :], (tgt, dist_s.shape[1]))
                    bias_s[h] = pltpu.roll(row, 0, 1, stride=1, stride_axis=0)[:, :tgt]

        def mask_scores(scores, h, b):
            allowed = causal & (dec_mask_ref[pl.ds(b, 1), :] > 0)
            return jnp.where(allowed, scores + bias_s[h], MASK_FILL)

        attend('self_attend', tgt, k_ref, v_ref, prepare, mask_scores)

    def cross_attention():
        def mask_scores(scores, h, b):
            return jnp.where(enc_mask_ref[pl.ds(b, 1), :] > 0, scores, MASK_FILL)

        attend('cross_attend', src, ck_ref, cv_ref, lambda g, b: None, mask_scores)

    hidden = big.at[:, pl.ds(0, width)]

    barrier = pltpu.get_barrier_semaphore()
    for j in range(1, N_DEV):
        pl.semaphore_signal(barrier, inc=1, device_id={'fsdp': me ^ j}, device_id_type=MESH)
    pl.semaphore_wait(barrier, N_DEV - 1)

    @pl.loop(0, AHEAD)
    def _(t):
        on_task(t, 0, AHEAD, send)

    def norm_copy(j):
        return pltpu.make_async_remote_copy(src_ref=norm_ref, dst_ref=gain_in.at[me], send_sem=norm_send.at[j], recv_sem=norm_recv.at[j],
                                            device_id={'fsdp': me ^ j}, device_id_type=MESH)

    for j in range(1, N_DEV):
        norm_copy(j).start()
    load(dec_ref, x_s)
    load(norm_ref, gain_in.at[me])
    table = jnp.zeros(dist_s.shape, F32)
    for b in range(NUM_BUCKETS):
        table = table + jnp.where(buckets_ref[...] == b, rel_ref[:, b:b + 1], 0.0)
    dist_s[...] = table
    for j in range(1, N_DEV):
        norm_copy(j).wait()
    per = width // N_DEV
    for d in range(N_DEV):
        gains[:, d * per:(d + 1) * per] = gain_in[d]

    plan = stage_ticks('head')

    @pl.loop(plan[0], plan[0] + plan[1])
    def _(i):
        tick(i, plan[0], plan[0] + plan[1])

    norm(0)
    project('self_q', 'self_q', q_ref)
    project('self_k', 'self_k', k_ref)
    project('self_v', 'self_v', v_ref)
    self_attention()
    load(c_ref, hidden)
    residual('self_o', 'self_o')
    for name, dst in (('cross_k', ck_ref), ('cross_v', cv_ref)):
        for half in range(2):
            load(enc_ref.at[pl.ds(half * rows, rows), :], hidden)
            project(name, f'{name}{half}', dst, half)
    norm(1)
    project('cross_q', 'cross_q', q_ref)
    cross_attention()
    load(c_ref, hidden)
    residual('cross_o', 'cross_o')
    norm(2)

    cols = weights['ff_gate'].width // 2
    block = pl.BlockSpec((rows, cols), lambda n: (0, n))

    def store_gate(total, span, n, g):
        g[span, :] = total.astype(BF16)

    def store_lin(total, span, n, g, z):
        act = jax.nn.gelu(g[span, :].astype(F32), approximate=True)
        z[span, :] = (act * total.astype(BF16).astype(F32)).astype(BF16)

    matmul('ff_gate', 'ff_gate', 2, store_gate, out_specs=[block], outs=[g_ref])
    matmul('ff_lin', 'ff_lin', 2, store_lin, in_specs=[block], ins=[g_ref], out_specs=[block], outs=[z_ref])
    load(z_ref, big)
    cols = weights['ff_out'].width

    def store_out(total, span, n, dst):
        where = (span, pl.ds(pl.multiple_of(n * cols, cols), cols))
        dst[span, :] = (x_s[where].astype(F32) + total.astype(BF16).astype(F32)).astype(BF16)

    matmul('ff_out', 'ff_out', 1, store_out, out_specs=[pl.BlockSpec((rows, cols), lambda n: (0, n))], outs=[out_ref])


def local_layer(dec_in, enc_out, dec_mask, enc_mask, rel_bias, norm_self, self_q, self_k, self_v, self_o, norm_cross, cross_q, cross_k, cross_v, cross_o, norm_ff, ff_gate, ff_lin, ff_out):
    batch, tgt, width = dec_in.shape
    src = enc_out.shape[1]
    rows = batch * tgt
    given = dict(self_q=self_q, self_k=self_k, self_v=self_v, self_o=self_o, cross_k=cross_k, cross_v=cross_v, cross_q=cross_q, cross_o=cross_o, ff_gate=ff_gate, ff_lin=ff_lin, ff_out=ff_out)
    names = list(TASKS)
    shards = [given[n] for n in names]
    lanes = -(-2 * tgt // 128) * 128 if tgt % 128 == 0 else -(-(tgt + 1) // 128) * 128
    norms = jnp.concatenate([jnp.stack([norm_self, norm_cross, norm_ff]).astype(F32), jnp.zeros((5, norm_self.shape[0]), F32)], 0)
    any_spec, vmem_spec = pl.BlockSpec(memory_space=pl.ANY), pl.BlockSpec(memory_space=pltpu.VMEM)
    hbm = lambda *shape: jax.ShapeDtypeStruct(shape, BF16)
    ff = ff_gate.shape[1]
    heads = rel_bias.shape[1]
    outs = [hbm(rows, width)] + [hbm(rows, width)] * 4 + [hbm(batch * src, width)] * 2 + [hbm(rows, ff)] * 2 + [hbm(N_DEV - 1, *s.shape) for s in shards]
    dma = pltpu.SemaphoreType.DMA
    flops = 2 * rows * width * (6 * width + 3 * ff) + 4 * batch * src * width * width
    result = pl.pallas_call(
        lambda *refs: layer_kernel(batch, names, *refs),
        out_shape=outs,
        in_specs=[vmem_spec] * 4 + [any_spec] * (3 + len(shards)),
        out_specs=[any_spec] * len(outs),
        scratch_shapes=[
            pltpu.VMEM((rows, width), BF16),
            pltpu.VMEM((rows, ff), BF16),
            pltpu.VMEM((min(GROUP, width) // HEAD_DIM, tgt, tgt), F32),
            pltpu.VMEM((heads, lanes), F32),
            pltpu.VMEM((N_DEV,) + norms.shape, F32),
            pltpu.VMEM((8, width), F32),
            dma((8, RING)), dma((8, RING)), dma((N_DEV,)), dma((N_DEV,)), dma(()),
        ],
        compiler_params=pltpu.CompilerParams(collective_id=0, has_side_effects=True, vmem_limit_bytes=67_043_328),
        cost_estimate=pl.CostEstimate(flops=flops, bytes_accessed=20 * sum(s.size for s in shards), transcendentals=0),
        name='layer',
    )(jnp.asarray(bucket_row(tgt, lanes)), rel_bias.T, dec_mask, enc_mask, norms, dec_in.reshape(rows, width), enc_out.reshape(batch * src, width), *shards)
    return result[0].reshape(dec_in.shape)


def solution(mesh):
    row_spec = P(('dp', 'fsdp'), None, None)
    mask_spec = P(('dp', 'fsdp'), None)
    weight_spec = P('fsdp', None)
    scale_spec = P('fsdp')
    in_specs = (row_spec, row_spec, mask_spec, mask_spec, P(None, None), scale_spec, weight_spec, weight_spec, weight_spec, weight_spec, scale_spec, weight_spec, weight_spec, weight_spec, weight_spec, scale_spec, weight_spec, weight_spec, weight_spec)
    return jax.shard_map(local_layer, mesh=mesh, in_specs=in_specs, out_specs=row_spec, check_vma=False)
```

time: 2550 us -> 2160 us (0.85)
  Pallas kernels: 0 us -> 2150 us
  matrix products: 1310 us -> 0 us
  waiting for transfers between devices: 874 us -> 0 us
  local copies, waits for them, and re-layouts: 286 us -> 14.1 us
  blocking collectives: 35.8 us -> 0 us
    pallas_call x0 -> x1, Pallas kernels: none -> 2150 us  [local_layer(): pl.pallas_call(lambda *refs: layer_kernel(batch, names, *refs), out_shape...]
    dot_general x13 -> x0, matrix products: 1180 us -> none  [the longest x11 1080 us: project(): jnp.einsum('btd,de->bte', hidden_in, weight, preferred_element_type=jnp.f...]
    all_gather x11 -> x0, waiting for transfers between devices: 867 us -> none  [gather_full(): return lax.all_gather(w_shard, 'fsdp', axis=0, tiled=True)]
    convert_element_type x6 -> x0, local copies, waits for them, and re-layouts: 144 us -> none  [project(): jnp.einsum('btd,de->bte', hidden_in, weight, preferred_element_type=jnp.f...]
    gather x3 -> x0, local copies, waits for them, and re-layouts: 142 us -> none  [the longest x2 141 us: self_bias(): bias_heads = jnp.take(per_offset, rel_dist, axis=1)]
    sub x2 -> x0, matrix products: 128 us -> none  [attend(): attn_prob = jax.nn.softmax(scores, axis=-1).astype(jnp.bfloat16)]
    all_gather x3 -> x0, blocking collectives: 35.8 us -> none  [gather_full(): return lax.all_gather(w_shard, 'fsdp', axis=0, tiled=True)]
  transfers between devices with their start and end apart: 11 -> 0, of which waited for: 8 -> 0; matrix products, arithmetic and copies ran while one was open for 58% -> 0% of each run, Pallas kernels for 0% -> 0%
where the time goes in v1:
time: 2160 us
  Pallas kernels  2150 us (100%)
    pallas_call x1, Pallas kernels, local_layer(): pl.pallas_call(lambda *refs: layer_kernel(batch, names, *refs), out_shape...  2150 us

profile of v1, /device:TPU:0, one launch (start us, length us, event | category | flops | bytes accessed | tf_op | source)
XLA Modules:
  0.0 2161.4 jit_solution(5699171271313710777)
XLA Ops:
  0.0 0.7 stack.12
  0.7 0.7 stack.13
  1.4 0.7 stack.14
  2.0 0.6 fusion.5.refs_4_
  2.7 1.4 copy.21
  4.1 2146.6 %layer.1 = (bf16[1536,4096]{1,0:T(8,128)(2,1)}, bf16[1536,4096]{1,0:T(8,128)(2,1)}, bf16[1536,4096]{1,0:T(8,128)(2,1)}, bf16[1536,4096]{1,0:T(8,128)(2,1)}, bf16...) custom-call(s32[1,256]{1,0:T(1,128)} %constant.5.clone.refs_0_, ...), custom_call_target="tpu_custom_call" | custom-call | flops 901943132160 | bytes 650117120 | tf_op jit(solution)/shard_map/layer/pallas_call | solution.py:337
  2150.7 10.7 copy.23

commit v2 on v1

--- a/solution.py
+++ b/solution.py
@@ -17,12 +17,12 @@
 MASK_FILL = -1e9
 N_DEV = 8
 
-AHEAD, PASS, DONE, RING = 4, 5, 6, 16
+AHEAD, PASS, DONE, RING, KINDS = 4, 4, 5, 16, 10
 TASKS = {'self_q': 8, 'self_k': 8, 'self_v': 8, 'self_o': 8, 'cross_k': 8, 'cross_v': 8, 'cross_q': 8, 'cross_o': 8, 'ff_gate': 20, 'ff_lin': 20, 'ff_out': 16}
 ALL_TASKS = sum(TASKS.values())
-TICKS = {'head': 8, 'self_q': 8, 'self_k': 8, 'self_v': 8, 'self_attend': 6, 'self_o': 6, 'cross_k0': 6, 'cross_k1': 5, 'cross_v0': 6, 'cross_v1': 5,
-         'cross_q': 6, 'cross_attend': 10, 'cross_o': 6, 'ff_gate': 13, 'ff_lin': 11, 'ff_out': 14}
-assert sum(TICKS.values()) == ALL_TASKS + DONE
+TICKS = {'head': DONE + 2, 'self_q': 8, 'self_k': 8, 'self_v': 8, 'self_attend': 6, 'self_o': 6, 'cross_k0': 6, 'cross_k1': 5, 'cross_v0': 6, 'cross_v1': 5,
+         'cross_q': 6, 'cross_attend': 10, 'cross_o': 6, 'ff_gate': 12, 'ff_lin': 10}
+assert sum(TICKS.values()) == ALL_TASKS - TASKS['ff_out'] + DONE
 ROW_BLOCK = 512
 GROUP = 512
 
@@ -31,9 +31,9 @@
     return [offset if offset < EXACT_BUCKETS else min(NUM_BUCKETS - 1, EXACT_BUCKETS + int(math.log(offset / EXACT_BUCKETS) / math.log(MAX_DISTANCE / EXACT_BUCKETS) * (NUM_BUCKETS - EXACT_BUCKETS))) for offset in range(length)]
 
 
-def bucket_row(length, lanes):
+def bucket_column(length, lanes):
     ids = bucket_ids(length)
-    return np.array([[ids[min((lanes - m) % lanes, length - 1)] for m in range(lanes)]], np.int32)
+    return np.array([[ids[min((lanes - m) % lanes, length - 1)]] for m in range(lanes)], np.int32)
 
 
 class Weight:
@@ -68,43 +68,59 @@
             cols = pl.ds(pl.multiple_of(m * w.width, w.width), w.width)
             own = w.shard.at[:, cols]
             slot = lambda j: w.got.at[j - 1, :, cols]
-            low = lambda j: w.got.at[j - 1, pl.ds(0, w.rows // 2), cols]
-            high = lambda j: w.got.at[j - 1, pl.ds(w.rows // 2, w.rows // 2), cols]
+            bottom, top = pl.ds(0, w.rows // 2), pl.ds(w.rows // 2, w.rows // 2)
+            low = lambda j: w.got.at[j - 1, bottom, cols]
+            high = lambda j: w.got.at[j - 1, top, cols]
             self.to_partner = lambda: remote(own, slot(1), 0, ring, 1)
-            self.to_x = lambda: remote(own, slot(2), 1, ring, 2)
-            self.to_y = lambda: remote(own, slot(4), 2, ring, 4)
-            self.relay_y = lambda: remote(low(2), low(6), 3, ring, 4)
-            self.relay_x = lambda: remote(high(4), high(6), 4, ring, 2)
-            self.swap_x = lambda: remote(slot(2), slot(3), 5, ring, 1)
-            self.swap_y = lambda: remote(slot(4), slot(5), 6, ring, 1)
-            self.swap_d = lambda: remote(slot(6), slot(7), 7, ring, 1)
+            self.first_x = lambda: remote(w.shard.at[bottom, cols], low(2), 1, ring, 2)
+            self.first_y = lambda: remote(w.shard.at[top, cols], high(4), 2, ring, 4)
+            self.rest_x = lambda: remote(w.shard.at[top, cols], high(2), 3, ring, 2)
+            self.rest_y = lambda: remote(w.shard.at[bottom, cols], low(4), 4, ring, 4)
+            self.relay_y = lambda: remote(low(2), low(6), 5, ring, 4)
+            self.relay_x = lambda: remote(high(4), high(6), 6, ring, 2)
+            self.swap_x = lambda: remote(slot(2), slot(3), 7, ring, 1)
+            self.swap_y = lambda: remote(slot(4), slot(5), 8, ring, 1)
+            self.swap_d = lambda: remote(slot(6), slot(7), 9, ring, 1)
 
     def send(t):
-        for copy in (t.to_x, t.to_y, t.to_partner):
+        for copy in (t.first_x, t.first_y, t.to_partner):
             copy().start()
 
     def arrive(t):
         t.to_partner().wait_recv()
-        t.to_x().wait_recv()
+        t.first_x().wait_recv()
         t.relay_y().start()
-        t.swap_x().start()
-        t.to_y().wait_recv()
+        t.rest_y().start()
+        t.first_y().wait_recv()
         t.relay_x().start()
-        t.swap_y().start()
-
-    def pass_on(t):
+        t.rest_x().start()
+
+    def pass_on_diagonal(t):
         t.relay_y().wait_recv()
         t.relay_x().wait_recv()
         t.swap_d().start()
 
+    def pass_on_rest(t):
+        t.rest_x().wait_recv()
+        t.swap_x().start()
+        t.rest_y().wait_recv()
+        t.swap_y().start()
+
+    def pass_on(t):
+        pass_on_diagonal(t)
+        pass_on_rest(t)
+
+    def wait_sends(t):
+        for copy in (t.to_partner, t.first_x, t.first_y, t.rest_x, t.rest_y, t.relay_y, t.relay_x, t.swap_x, t.swap_y, t.swap_d):
+            copy().wait_send()
+
     def finish(t):
         for copy in (t.swap_x, t.swap_y, t.swap_d):
-            copy().wait()
-        for copy in (t.to_partner, t.to_x, t.to_y, t.relay_y, t.relay_x):
-            copy().wait_send()
-
-    def on_task(t, low, high, act):
-        for w in weights.values():
+            copy().wait_recv()
+        wait_sends(t)
+
+    def on_task(t, low, high, act, among=None):
+        for w in among or weights.values():
             if low < w.first + w.count and w.first < high:
                 def run(w=w):
                     act(Task(w, t - w.first, lax.rem(t, RING)))
@@ -116,8 +132,9 @@
     def tick(i, low, high):
         on_task(i, low, high, arrive)
         on_task(i + AHEAD, low + AHEAD, high + AHEAD, send)
-        on_task(i - PASS, low - PASS, high - PASS, pass_on)
-        on_task(i - DONE, low - DONE, high - DONE, finish)
+        streamed = [w for name, w in weights.items() if name != 'ff_out']
+        on_task(i - PASS, low - PASS, high - PASS, pass_on, streamed)
+        on_task(i - DONE, low - DONE, high - DONE, finish, streamed)
 
     done = [0]
 
@@ -126,16 +143,16 @@
         done[0] = low + count
         return low, count
 
-    def run_ticks(plan, n, steps, one_each=False):
+    def ticks_before(plan, n, steps, least=min):
         low, count = plan
-        if one_each:
-            begin, end = jnp.minimum(low + n, low + count), jnp.minimum(low + n + 1, low + count)
-        else:
-            begin, end = low + (n * count) // steps, low + ((n + 1) * count) // steps
-
-        @pl.loop(begin, end)
-        def _(i):
-            tick(i, low, low + count)
+        spread = steps if count == steps else max(steps - 4, 1)
+        return low + least((n * count) // spread, count)
+
+    def run_ticks(plan, n, steps):
+        with jax.named_scope('ticks'):
+            @pl.loop(ticks_before(plan, n, steps, jnp.minimum), ticks_before(plan, n + 1, steps, jnp.minimum))
+            def _(i):
+                tick(i, plan[0], plan[0] + plan[1])
 
     def load(src_ref, dst_ref):
         copy = pltpu.make_async_copy(src_ref, dst_ref, load_sem)
@@ -154,6 +171,8 @@
         w = weights[name]
         steps, cols = w.count * split, w.width // split
         plan = stage_ticks(stage)
+        for n in range(steps):
+            assert ticks_before(plan, n, steps) > w.first + min(n + 1, steps - 1) // split + DONE
 
         def body(own, got, *rest):
             n = pl.program_id(0)
@@ -168,12 +187,13 @@
                     total = term if total is None else total + term
                 store(total, span, n, *rest)
 
-            run_ticks(plan, n, steps, stage == 'ff_out')
-
-        pltpu.emit_pipeline(
-            body, grid=(steps,),
-            in_specs=[pl.BlockSpec((w.rows, cols), lambda n: (0, n)), pl.BlockSpec((N_DEV - 1, w.rows, cols), lambda n: (0, 0, n)), *in_specs],
-            out_specs=list(out_specs))(w.shard, w.got, *ins, *outs)
+            run_ticks(plan, n, steps)
+
+        with jax.named_scope(stage):
+            pltpu.emit_pipeline(
+                body, grid=(steps,),
+                in_specs=[pl.BlockSpec((w.rows, cols), lambda n: (0, n)), pl.BlockSpec((N_DEV - 1, w.rows, cols), lambda n: (0, 0, n)), *in_specs],
+                out_specs=list(out_specs))(w.shard, w.got, *ins, *outs)
 
     def project(name, stage, dst_ref, half=0):
         cols = weights[name].width
@@ -217,7 +237,8 @@
             run_ticks(plan, g * batch + b, steps)
 
         spec = lambda length: pl.BlockSpec((length, group), lambda g, b: (b, g))
-        pltpu.emit_pipeline(body, grid=(width // group, batch), in_specs=[spec(tgt), spec(keys), spec(keys)], out_specs=[spec(tgt)])(q_ref, k_src, v_src, c_ref)
+        with jax.named_scope(stage):
+            pltpu.emit_pipeline(body, grid=(width // group, batch), in_specs=[spec(tgt), spec(keys), spec(keys)], out_specs=[spec(tgt)])(q_ref, k_src, v_src, c_ref)
 
     def self_attention():
         heads = min(GROUP, width) // HEAD_DIM
@@ -262,10 +283,10 @@
         norm_copy(j).start()
     load(dec_ref, x_s)
     load(norm_ref, gain_in.at[me])
-    table = jnp.zeros(dist_s.shape, F32)
+    table = jnp.zeros((buckets_ref.shape[0], rel_ref.shape[1]), F32)
     for b in range(NUM_BUCKETS):
-        table = table + jnp.where(buckets_ref[...] == b, rel_ref[:, b:b + 1], 0.0)
-    dist_s[...] = table
+        table = table + jnp.where(buckets_ref[...] == b, rel_ref[b:b + 1, :], 0.0)
+    dist_s[...] = table.T
     for j in range(1, N_DEV):
         norm_copy(j).wait()
     per = width // N_DEV
@@ -273,10 +294,10 @@
         gains[:, d * per:(d + 1) * per] = gain_in[d]
 
     plan = stage_ticks('head')
-
-    @pl.loop(plan[0], plan[0] + plan[1])
-    def _(i):
-        tick(i, plan[0], plan[0] + plan[1])
+    with jax.named_scope('head'):
+        @pl.loop(plan[0], plan[0] + plan[1])
+        def _(i):
+            tick(i, plan[0], plan[0] + plan[1])
 
     norm(0)
     project('self_q', 'self_q', q_ref)
@@ -309,13 +330,79 @@
     matmul('ff_gate', 'ff_gate', 2, store_gate, out_specs=[block], outs=[g_ref])
     matmul('ff_lin', 'ff_lin', 2, store_lin, in_specs=[block], ins=[g_ref], out_specs=[block], outs=[z_ref])
     load(z_ref, big)
-    cols = weights['ff_out'].width
-
-    def store_out(total, span, n, dst):
-        where = (span, pl.ds(pl.multiple_of(n * cols, cols), cols))
-        dst[span, :] = (x_s[where].astype(F32) + total.astype(BF16).astype(F32)).astype(BF16)
-
-    matmul('ff_out', 'ff_out', 1, store_out, out_specs=[pl.BlockSpec((rows, cols), lambda n: (0, n))], outs=[out_ref])
+    w = weights['ff_out']
+    last = w.first + w.count
+
+    def ff_out_loop(early, late, total, outs, early_sem, late_sem, out_sem):
+        cols = w.width
+
+        def span_of(m):
+            return pl.ds(pl.multiple_of(m * row_block, row_block), row_block)
+
+        def product(span, buf, slots):
+            terms = [jnp.dot(big[span, pl.ds(pl.multiple_of((me ^ j) * w.rows, 128), w.rows)], buf[p], preferred_element_type=F32) for p, j in enumerate(slots)]
+            return sum(terms[1:], terms[0])
+
+        @pl.loop(0, w.count)
+        def _(n):
+            where = pl.ds(pl.multiple_of(n * cols, cols), cols)
+            t = Task(w, n, lax.rem(w.first + n, RING))
+
+            def fetch(j, buf, p, sem):
+                return pltpu.make_async_copy(w.shard.at[:, where] if j == 0 else w.got.at[j - 1, :, where], buf.at[p], sem.at[p])
+
+            def out_copy(k):
+                return pltpu.make_async_copy(outs.at[lax.rem(k, 2)], out_ref.at[:, pl.ds(pl.multiple_of(k * cols, cols), cols)], out_sem.at[lax.rem(k, 2)])
+
+            first, second = (0, 1, 6, 7), (2, 4, 3, 5)
+            for p in (0, 1):
+                fetch(first[p], early, p, early_sem).start()
+            pass_on_diagonal(t)
+            fetch(6, early, 2, early_sem).start()
+            t.swap_d().wait_recv()
+            fetch(7, early, 3, early_sem).start()
+            for p, j in enumerate(first):
+                fetch(j, early, p, early_sem).wait()
+
+            @pl.loop(0, rows // row_block)
+            def _(m):
+                total[span_of(m), :] = product(span_of(m), early, first)
+
+            @pl.when(n >= 2)
+            def _():
+                out_copy(n - 2).wait()
+
+            pass_on_rest(t)
+            for p in (0, 1):
+                fetch(second[p], late, p, late_sem).start()
+            t.swap_x().wait_recv()
+            fetch(3, late, 2, late_sem).start()
+            t.swap_y().wait_recv()
+            fetch(5, late, 3, late_sem).start()
+            for p, j in enumerate(second):
+                fetch(j, late, p, late_sem).wait()
+
+            @pl.loop(0, rows // row_block)
+            def _(m):
+                span = span_of(m)
+                update = (total[span, :] + product(span, late, second)).astype(BF16)
+                outs[lax.rem(n, 2), span, :] = (x_s[span, where].astype(F32) + update.astype(F32)).astype(BF16)
+
+            out_copy(n).start()
+            wait_sends(t)
+            begin = w.first + DONE
+            on_task(begin + n, begin, last + DONE, arrive, [w])
+            on_task(begin + AHEAD + n, begin + AHEAD, last + DONE + AHEAD, send, [w])
+
+            @pl.when(n == w.count - 1)
+            def _():
+                out_copy(n - 1).wait()
+                out_copy(n).wait()
+
+    dma = pltpu.SemaphoreType.DMA
+    with jax.named_scope('ff_out'):
+        pl.run_scoped(ff_out_loop, pltpu.VMEM((4, w.rows, w.width), BF16), pltpu.VMEM((4, w.rows, w.width), BF16), pltpu.VMEM((rows, w.width), F32),
+                      pltpu.VMEM((2, rows, w.width), BF16), dma((4,)), dma((4,)), dma((2,)))
 
 
 def local_layer(dec_in, enc_out, dec_mask, enc_mask, rel_bias, norm_self, self_q, self_k, self_v, self_o, norm_cross, cross_q, cross_k, cross_v, cross_o, norm_ff, ff_gate, ff_lin, ff_out):
@@ -326,7 +413,8 @@
     names = list(TASKS)
     shards = [given[n] for n in names]
     lanes = -(-2 * tgt // 128) * 128 if tgt % 128 == 0 else -(-(tgt + 1) // 128) * 128
-    norms = jnp.concatenate([jnp.stack([norm_self, norm_cross, norm_ff]).astype(F32), jnp.zeros((5, norm_self.shape[0]), F32)], 0)
+    which = lax.broadcasted_iota(jnp.int32, (8, norm_self.shape[0]), 0)
+    norms = jnp.where(which == 0, norm_self[None], jnp.where(which == 1, norm_cross[None], norm_ff[None])).astype(F32)
     any_spec, vmem_spec = pl.BlockSpec(memory_space=pl.ANY), pl.BlockSpec(memory_space=pltpu.VMEM)
     hbm = lambda *shape: jax.ShapeDtypeStruct(shape, BF16)
     ff = ff_gate.shape[1]
@@ -346,12 +434,12 @@
             pltpu.VMEM((heads, lanes), F32),
             pltpu.VMEM((N_DEV,) + norms.shape, F32),
             pltpu.VMEM((8, width), F32),
-            dma((8, RING)), dma((8, RING)), dma((N_DEV,)), dma((N_DEV,)), dma(()),
+            dma((KINDS, RING)), dma((KINDS, RING)), dma((N_DEV,)), dma((N_DEV,)), dma(()),
         ],
         compiler_params=pltpu.CompilerParams(collective_id=0, has_side_effects=True, vmem_limit_bytes=67_043_328),
         cost_estimate=pl.CostEstimate(flops=flops, bytes_accessed=20 * sum(s.size for s in shards), transcendentals=0),
         name='layer',
-    )(jnp.asarray(bucket_row(tgt, lanes)), rel_bias.T, dec_mask, enc_mask, norms, dec_in.reshape(rows, width), enc_out.reshape(batch * src, width), *shards)
+    )(jnp.asarray(bucket_column(tgt, lanes)), rel_bias, dec_mask, enc_mask, norms, dec_in.reshape(rows, width), enc_out.reshape(batch * src, width), *shards)
     return result[0].reshape(dec_in.shape)
 
 

time: 2160 us -> 2140 us (level)
  no operation moved by 1% of the time
where the time goes in v2:
time: 2140 us
  Pallas kernels  2130 us (100%)
    pallas_call x1, Pallas kernels, local_layer(): pl.pallas_call(lambda *refs: layer_kernel(batch, names, *refs), out_shape...  2130 us

profile of v2, /device:TPU:0, one launch (start us, length us, event | category | flops | bytes accessed | tf_op | source)
XLA Modules:
  0.0 2141.0 jit_solution(3812515579955314008)
XLA Ops:
  0.0 1.4 select_convert_fusion.refs_4_
  1.4 2128.9 %layer.1 = (bf16[1536,4096]{1,0:T(8,128)(2,1)}, bf16[1536,4096]{1,0:T(8,128)(2,1)}, bf16[1536,4096]{1,0:T(8,128)(2,1)}, bf16[1536,4096]{1,0:T(8,128)(2,1)}, bf16...) custom-call(s32[256,1]{1,0:T(8,128)} %constant.6.clone.refs_0_, ...), custom_call_target="tpu_custom_call" | custom-call | flops 901943132160 | bytes 650117120 | tf_op jit(solution)/shard_map/layer/pallas_call | solution.py:425
  2130.3 10.7 copy.22
  (1 shorter events, 0.0 us)
